TPU v7x, 32 devices: a whole 2x2x4 slice. The times are simulated.
32 devices in a mesh: row: 8 (over y, x, core), col: 4 (over z).
Axes of the slice: x: 2, y: 2, z: 4, core: 2. Of those that a mesh axis runs over, the one named last changes fastest.
Arguments:
- history: float32 [3, 512, 4096], P(None, None, ('row', 'col')), may hold values from -8 to 8
Outputs:
- orbitals: float32 [512, 4096], P(None, ('row', 'col'))
All inputs are finite; a program needn't handle non-finite values.
Results may differ from a plain program's by a relative error of at most 0.0003.
Values sent between devices are 32-bit elements; how exact they have to be, the bound alone decides.
A program may use at most 64 MiB of HBM per device.

v0:
```python
import jax
import jax.numpy as jnp
from jax import lax
from jax.sharding import PartitionSpec as P


def on_device(history):
    precise = lax.Precision.HIGHEST
    npw_total = history.shape[2] * lax.axis_size("row") * lax.axis_size("col")
    newest = history[0]
    local_terms = tuple(
        (jnp.einsum("ip,jp->ij", newest, history[index], precision=precise) for index in range(3))
    )
    summed = lax.psum(local_terms, ("row", "col"))
    weights = (2.5, -2.0, 0.5)
    predicted = jnp.zeros(newest.shape, jnp.float32)
    for index in range(3):
        project = summed[index] / npw_total
        predicted = predicted + weights[index] * jnp.dot(project, history[index], precision=precise)
    local_gram = jnp.einsum("ip,jp->ij", predicted, predicted, precision=precise)
    gram = lax.psum(local_gram, ("row", "col"))
    factor = jnp.linalg.cholesky(gram / npw_total)
    return lax.linalg.triangular_solve(factor, predicted, left_side=True, lower=True)


def solution(mesh):
    return jax.shard_map(
        on_device,
        mesh=mesh,
        in_specs=(P(None, None, ("row", "col")),),
        out_specs=P(None, ("row", "col")),
        check_vma=False,
    )
```

profile of v0, /device:TPU:0, one launch (start us, length us, event | category | flops | bytes accessed | tf_op | source)
XLA Modules:
  0.0 441.3 jit_solution(1607792850113480831)
XLA Ops:
  6.5 3.1 fusion.11
  9.7 2.0 fusion.14
  11.6 2.0 fusion.19
  13.6 0.5 all-reduce.5.cloned.1.call-start
  14.1 141.3 %all-reduce.7.cloned.1.call-done = (f32[512,512]{0,1:T(8,128)}, f32[512,512]{0,1:T(8,128)}, f32[512,512]{0,1:T(8,128)}) async-done(((f32[512,512]{0,1:T(8,128)}, f32[512,512]{0,1:T(8,128)}, f32[512,512]{0,1:T(8,128)}), (f32[512,512]{0,1:T(8,128)}, f32[512,512]{0,1:T(8,128)}, f32[512,512]{0,1:T(8,128)})) %all-reduce.7.cloned.1.call-update) | async-done | bytes 3145744 | tf_op jit(solution)/shard_map/psum | solution.py:14
  155.4 3.1 convolution_multiply_fusion.2
  158.6 1.8 fusion.1
  160.4 1.8 fusion
  162.2 2.0 fusion.61
  164.3 130.2 %all-reduce.5.cloned.1.call-done = f32[512,512]{0,1:T(8,128)} async-done(((f32[512,512]{0,1:T(8,128)}), f32[512,512]{0,1:T(8,128)}) %all-reduce.5.cloned.1.call-update) | async-done | bytes 1048592 | tf_op jit(solution)/shard_map/psum | solution.py:21
  294.5 1.3 broadcast_multiply_fusion
  295.8 0.3 copy.3
  296.2 0.9 copy-done.1
  297.0 0.2 fusion.2
  297.3 11.7 %cholesky.104 = f32[128,128]{1,0:T(8,128)S(1)} custom-call(f32[128,128]{1,0:T(8,128)S(1)} %cholesky.266), custom_call_target="Cholesky" | custom-call | tf_op jit(solution)/shard_map/jit(cholesky)/cholesky | solution.py:22
  309.0 10.0 %custom-call.30 = f32[1,128,128]{1,2,0:T(8,128)S(1)} custom-call(f32[1,128,128]{2,1,0:T(8,128)S(1)} %get-tuple-element.35), custom_call_target="InvertDiagBlocksLowerTriangular" | custom-call | tf_op jit(solution)/shard_map/jit(cholesky)/cholesky | solution.py:22
  319.1 0.3 constant_dynamic-update-slice_fusion.3
  319.4 0.3 convolution_subtract_fusion
  319.8 11.7 %cholesky.217 = f32[128,128]{1,0:T(8,128)S(1)} custom-call(f32[128,128]{1,0:T(8,128)S(1)} %cholesky.270), custom_call_target="Cholesky" | custom-call | tf_op jit(solution)/shard_map/jit(cholesky)/cholesky | solution.py:22
  331.5 9.8 %custom-call.31 = f32[1,128,128]{1,2,0:T(8,128)S(1)} custom-call(f32[1,128,128]{2,1,0:T(8,128)S(1)} %get-tuple-element.32), custom_call_target="InvertDiagBlocksLowerTriangular" | custom-call | tf_op jit(solution)/shard_map/jit(cholesky)/cholesky | solution.py:22
  341.4 0.3 convolution_dynamic-update-slice_fusion
  341.6 0.4 convolution_subtract_fusion.1
  342.0 11.7 %cholesky.238 = f32[128,128]{1,0:T(8,128)S(1)} custom-call(f32[128,128]{1,0:T(8,128)S(1)} %cholesky.275), custom_call_target="Cholesky" | custom-call | tf_op jit(solution)/shard_map/jit(cholesky)/cholesky | solution.py:22
  353.8 0.7 compare_reduce_fusion.1
  354.5 10.0 %custom-call.32 = f32[1,128,128]{1,2,0:T(8,128)S(1)} custom-call(f32[1,128,128]{2,1,0:T(8,128)S(1)} %get-tuple-element.29), custom_call_target="InvertDiagBlocksLowerTriangular" | custom-call | tf_op jit(solution)/shard_map/jit(cholesky)/cholesky | solution.py:22
  364.5 0.2 convolution_dynamic-update-slice_fusion.1
  364.7 0.4 convolution_subtract_fusion.5
  365.1 11.7 %cholesky.255 = f32[128,128]{1,0:T(8,128)S(1)} custom-call(f32[128,128]{1,0:T(8,128)S(1)} %convolution_subtract_fusion.5), custom_call_target="Cholesky" | custom-call | tf_op jit(solution)/shard_map/jit(cholesky)/cholesky | solution.py:22
  376.8 0.6 compare_reduce_fusion
  377.5 0.7 compare_reduce_fusion.2
  380.8 10.6 %while.1 = (s32[]{:T(128)}, f32[512,512]{1,0:T(8,128)S(1)}, s32[4,2]{0,1:T(2,128)S(1)}, f32[4,128,128]{2,1,0:T(8,128)}, s32[]{:T(128)}) while((s32[]{:T(128)}, f32[512,512]{1,0:T(8,128)S(1)}, s32[4,2]{0,1:T(2,128)S(1)}, f32[4,128,128]{2,1,0:T(8,128)}, s32[]{:T(128)}) %tuple.27), condition=%wide.while_cond, body=%wide.while_body.sunk | while | flops 2 | bytes 132705 | solution.py:23
  380.9 0.6 fusion.70
  381.5 2.0 bitcast_dynamic-update-slice_fusion.2
  383.6 0.6 fusion.70
  384.2 2.0 bitcast_dynamic-update-slice_fusion.2
  386.2 0.6 fusion.70
  386.8 2.0 bitcast_dynamic-update-slice_fusion.2
  388.9 0.6 fusion.70
  389.5 2.0 bitcast_dynamic-update-slice_fusion.2
  391.4 40.1 %custom-call.33 = f32[4,128,128]{1,2,0:T(8,128)S(1)} custom-call(f32[4,128,128]{2,1,0:T(8,128)} %get-tuple-element.12), custom_call_target="InvertDiagBlocksLowerTriangular" | custom-call | tf_op jit(solution)/shard_map/triangular_solve | solution.py:23
  431.6 0.3 fusion.48
  431.9 0.2 convolution_subtract_fusion.3
  432.1 0.3 fusion.47
  432.4 0.3 convolution_subtract_fusion.2
  432.6 0.3 fusion.45
  432.9 0.3 convolution_subtract_fusion.4
  433.3 0.3 fusion.44
  433.5 0.7 pad_maximum_fusion
  (26 shorter events, 0.8 us)
Async XLA Ops:
  6.5 3.1 copy-start
  6.5 148.9 %all-reduce.7.cloned.1.call-start = ((), (), s32[]{:S(2)}) async-start(), calls=%async_computation.1 | async-start | bytes 6291456 | tf_op jit(solution)/shard_map/psum | solution.py:14
  13.6 280.9 %all-reduce.5.cloned.1.call-start = ((), (), s32[]{:S(2)}) async-start(), calls=%async_computation | async-start | bytes 2097152 | tf_op jit(solution)/shard_map/psum | solution.py:21
  155.4 3.1 copy-start.3
  158.5 1.8 copy-start.2
  295.8 1.2 copy-start.1
Sparse Core Ops, SparseCore 0:
  13.8 141.6 all-reduce.6
  164.4 130.0 all-reduce.4
where the time goes:
time: 444 us; the launch traced here: 441 us
  waiting for transfers between devices  271 us (61%)
  other arithmetic  121 us (27%)
  matrix products  19.7 us (4%)
  between operations  16.4 us (4%)
  local copies, waits for them, and re-layouts  11.9 us (3%)
    psum x1, waiting for transfers between devices, on_device(): summed = lax.psum(local_terms, ('row', 'col'))  141 us
    psum x1, waiting for transfers between devices, on_device(): gram = lax.psum(local_gram, ('row', 'col'))  130 us
    another operation x14, other arithmetic, on_device(): factor = jnp.linalg.cholesky(gram / npw_total)  78.8 us
    another operation x4, other arithmetic, on_device(): lax.linalg.triangular_solve(factor, predicted, left_side=True, lower=True)  41 us
    another operation x12, local copies, waits for them, and re-layouts  10.6 us
  transfers between devices with their start and end apart: 2, of which 2 were waited for; matrix products, arithmetic and copies ran while one was open for 0% of the time, Pallas kernels for 0%

commit v1 on v0

--- a/solution.py
+++ b/solution.py
@@ -1,7 +1,16 @@
+import functools
 import jax
 import jax.numpy as jnp
 from jax import lax
 from jax.sharding import PartitionSpec as P
+from jax.lax import psum
+
+
+def waves_press(m, bus_axis, mesh_name):
+    return psum(psum(m, bus_axis), mesh_name)
+
+
+carry_inputs = functools.partial(waves_press, bus_axis="col", mesh_name="row")
 
 
 def on_device(history):
@@ -11,7 +20,7 @@
     local_terms = tuple(
         (jnp.einsum("ip,jp->ij", newest, history[index], precision=precise) for index in range(3))
     )
-    summed = lax.psum(local_terms, ("row", "col"))
+    summed = carry_inputs(local_terms)
     weights = (2.5, -2.0, 0.5)
     predicted = jnp.zeros(newest.shape, jnp.float32)
     for index in range(3):

time: 444 us -> 499 us (1.12)
  waiting for transfers between devices: 271 us -> 326 us
    psum x1 -> x2, waiting for transfers between devices: 141 us -> 195 us  [waves_press(): return psum(psum(m, bus_axis), mesh_name)]
  transfers between devices with their start and end apart: 2 -> 3, of which waited for: 2 -> 3; matrix products, arithmetic and copies ran while one was open for 0% -> 0% of each run, Pallas kernels for 0% -> 0%
where the time goes in v1:
time: 499 us; the launch traced here: 496 us
  waiting for transfers between devices  326 us (65%)
  other arithmetic  121 us (24%)
  matrix products  19.7 us (4%)
  between operations  16.1 us (3%)
  local copies, waits for them, and re-layouts  11.9 us (2%)
    psum x2, waiting for transfers between devices, waves_press(): return psum(psum(m, bus_axis), mesh_name)  195 us
    psum x1, waiting for transfers between devices, on_device(): gram = lax.psum(local_gram, ('row', 'col'))  131 us
    another operation x14, other arithmetic, on_device(): factor = jnp.linalg.cholesky(gram / npw_total)  78.8 us
    another operation x4, other arithmetic, on_device(): lax.linalg.triangular_solve(factor, predicted, left_side=True, lower=True)  41 us
    another operation x12, local copies, waits for them, and re-layouts  10.6 us
  transfers between devices with their start and end apart: 3, of which 3 were waited for; matrix products, arithmetic and copies ran while one was open for 0% of the time, Pallas kernels for 0%

profile of v1, /device:TPU:0, one launch (start us, length us, event | category | flops | bytes accessed | tf_op | source)
XLA Modules:
  0.0 496.1 jit_solution(16473956735357557848)
XLA Ops:
  6.5 3.1 fusion.11
  9.7 2.0 fusion.14
  11.6 2.0 fusion.19
  13.7 123.9 %all-reduce.11.cloned.1.call-done = (f32[512,512]{0,1:T(8,128)}, f32[512,512]{0,1:T(8,128)}, f32[512,512]{0,1:T(8,128)}) async-done(((f32[512,512]{0,1:T(8,128)}, f32[512,512]{0,1:T(8,128)}, f32[512,512]{0,1:T(8,128)}), (f32[512,512]{0,1:T(8,128)}, f32[512,512]{0,1:T(8,128)}, f32[512,512]{0,1:T(8,128)})) %all-reduce.11.cloned.1.call-update) | async-done | bytes 3145744 | tf_op jit(solution)/shard_map/psum | solution.py:10
  137.6 0.5 all-reduce.7.cloned.1.call-start
  138.1 71.6 %all-reduce.9.cloned.1.call-done = (f32[512,512]{0,1:T(8,128)}, f32[512,512]{0,1:T(8,128)}, f32[512,512]{0,1:T(8,128)}) async-done(((f32[512,512]{0,1:T(8,128)}, f32[512,512]{0,1:T(8,128)}, f32[512,512]{0,1:T(8,128)}), (f32[512,512]{0,1:T(8,128)}, f32[512,512]{0,1:T(8,128)}, f32[512,512]{0,1:T(8,128)})) %all-reduce.9.cloned.1.call-update) | async-done | bytes 3145744 | tf_op jit(solution)/shard_map/psum | solution.py:10
  209.7 3.1 convolution_multiply_fusion.2
  212.8 1.8 fusion.1
  214.7 1.8 fusion
  216.5 2.0 fusion.61
  218.6 131.0 %all-reduce.7.cloned.1.call-done = f32[512,512]{0,1:T(8,128)} async-done(((f32[512,512]{0,1:T(8,128)}), f32[512,512]{0,1:T(8,128)}) %all-reduce.7.cloned.1.call-update) | async-done | bytes 1048592 | tf_op jit(solution)/shard_map/psum | solution.py:30
  349.6 1.3 broadcast_multiply_fusion
  350.9 0.3 copy.3
  351.2 0.9 copy-done.1
  352.1 0.2 fusion.2
  352.4 11.7 %cholesky.104 = f32[128,128]{1,0:T(8,128)S(1)} custom-call(f32[128,128]{1,0:T(8,128)S(1)} %cholesky.266), custom_call_target="Cholesky" | custom-call | tf_op jit(solution)/shard_map/jit(cholesky)/cholesky | solution.py:31
  364.1 10.0 %custom-call.30 = f32[1,128,128]{1,2,0:T(8,128)S(1)} custom-call(f32[1,128,128]{2,1,0:T(8,128)S(1)} %get-tuple-element.38), custom_call_target="InvertDiagBlocksLowerTriangular" | custom-call | tf_op jit(solution)/shard_map/jit(cholesky)/cholesky | solution.py:31
  374.2 0.3 constant_dynamic-update-slice_fusion.3
  374.5 0.3 convolution_subtract_fusion
  374.9 11.7 %cholesky.217 = f32[128,128]{1,0:T(8,128)S(1)} custom-call(f32[128,128]{1,0:T(8,128)S(1)} %cholesky.270), custom_call_target="Cholesky" | custom-call | tf_op jit(solution)/shard_map/jit(cholesky)/cholesky | solution.py:31
  386.6 9.8 %custom-call.31 = f32[1,128,128]{1,2,0:T(8,128)S(1)} custom-call(f32[1,128,128]{2,1,0:T(8,128)S(1)} %get-tuple-element.35), custom_call_target="InvertDiagBlocksLowerTriangular" | custom-call | tf_op jit(solution)/shard_map/jit(cholesky)/cholesky | solution.py:31
  396.4 0.3 convolution_dynamic-update-slice_fusion
  396.7 0.4 convolution_subtract_fusion.1
  397.1 11.7 %cholesky.238 = f32[128,128]{1,0:T(8,128)S(1)} custom-call(f32[128,128]{1,0:T(8,128)S(1)} %cholesky.275), custom_call_target="Cholesky" | custom-call | tf_op jit(solution)/shard_map/jit(cholesky)/cholesky | solution.py:31
  408.9 0.7 compare_reduce_fusion.1
  409.6 10.0 %custom-call.32 = f32[1,128,128]{1,2,0:T(8,128)S(1)} custom-call(f32[1,128,128]{2,1,0:T(8,128)S(1)} %get-tuple-element.32), custom_call_target="InvertDiagBlocksLowerTriangular" | custom-call | tf_op jit(solution)/shard_map/jit(cholesky)/cholesky | solution.py:31
  419.8 0.4 convolution_subtract_fusion.5
  420.2 11.7 %cholesky.255 = f32[128,128]{1,0:T(8,128)S(1)} custom-call(f32[128,128]{1,0:T(8,128)S(1)} %convolution_subtract_fusion.5), custom_call_target="Cholesky" | custom-call | tf_op jit(solution)/shard_map/jit(cholesky)/cholesky | solution.py:31
  431.9 0.6 compare_reduce_fusion
  432.6 0.7 compare_reduce_fusion.2
  435.9 10.6 %while.1 = (s32[]{:T(128)}, f32[512,512]{1,0:T(8,128)S(1)}, s32[4,2]{0,1:T(2,128)S(1)}, f32[4,128,128]{2,1,0:T(8,128)}, s32[]{:T(128)}) while((s32[]{:T(128)}, f32[512,512]{1,0:T(8,128)S(1)}, s32[4,2]{0,1:T(2,128)S(1)}, f32[4,128,128]{2,1,0:T(8,128)}, s32[]{:T(128)}) %tuple.27), condition=%wide.while_cond, body=%wide.while_body.sunk | while | flops 2 | bytes 132705 | solution.py:32
  436.0 0.6 fusion.70
  436.6 2.0 bitcast_dynamic-update-slice_fusion.2
  438.7 0.6 fusion.70
  439.3 2.0 bitcast_dynamic-update-slice_fusion.2
  441.3 0.6 fusion.70
  441.9 2.0 bitcast_dynamic-update-slice_fusion.2
  443.9 0.6 fusion.70
  444.5 2.0 bitcast_dynamic-update-slice_fusion.2
  446.5 40.1 %custom-call.33 = f32[4,128,128]{1,2,0:T(8,128)S(1)} custom-call(f32[4,128,128]{2,1,0:T(8,128)} %get-tuple-element.12), custom_call_target="InvertDiagBlocksLowerTriangular" | custom-call | tf_op jit(solution)/shard_map/triangular_solve | solution.py:32
  486.6 0.3 fusion.48
  486.9 0.2 convolution_subtract_fusion.3
  487.2 0.3 fusion.47
  487.4 0.3 convolution_subtract_fusion.2
  487.7 0.3 fusion.45
  488.0 0.3 convolution_subtract_fusion.4
  488.3 0.3 fusion.44
  488.6 0.7 pad_maximum_fusion
  (29 shorter events, 1.0 us)
Async XLA Ops:
  6.5 3.1 copy-start
  6.5 131.1 %all-reduce.11.cloned.1.call-start = ((), (), s32[]{:S(2)}) async-start(), calls=%async_computation.2 | async-start | bytes 6291456 | tf_op jit(solution)/shard_map/psum | solution.py:10
  13.6 196.1 %all-reduce.9.cloned.1.call-start = ((), (), s32[]{:S(2)}) async-start(), calls=%async_computation.1 | async-start | bytes 6291456 | tf_op jit(solution)/shard_map/psum | solution.py:10
  137.6 211.9 %all-reduce.7.cloned.1.call-start = ((), (), s32[]{:S(2)}) async-start(), calls=%async_computation | async-start | bytes 2097152 | tf_op jit(solution)/shard_map/psum | solution.py:30
  209.7 3.1 copy-start.3
  212.8 1.9 copy-start.2
  350.9 1.2 copy-start.1
Sparse Core Ops, SparseCore 0:
  13.8 123.8 all-reduce.10
  141.2 68.4 all-reduce.8
  218.7 130.8 all-reduce.6

commit v2 on v0

--- a/solution.py
+++ b/solution.py
@@ -18,7 +18,8 @@
         project = summed[index] / npw_total
         predicted = predicted + weights[index] * jnp.dot(project, history[index], precision=precise)
     local_gram = jnp.einsum("ip,jp->ij", predicted, predicted, precision=precise)
-    gram = lax.psum(local_gram, ("row", "col"))
+    pieces = lax.all_gather(local_gram, ("row", "col"), axis=0, tiled=False)
+    gram = pieces.sum(axis=0)
     factor = jnp.linalg.cholesky(gram / npw_total)
     return lax.linalg.triangular_solve(factor, predicted, left_side=True, lower=True)
 

time: 444 us -> 517 us (1.16)
  waiting for transfers between devices: 271 us -> 335 us
  other arithmetic: 121 us -> 132 us
    all_gather x0 -> x1, waiting for transfers between devices: none -> 194 us  [on_device(): pieces = lax.all_gather(local_gram, ('row', 'col'), axis=0, tiled=False)]
    psum x1 -> x0, waiting for transfers between devices: 130 us -> none  [on_device(): gram = lax.psum(local_gram, ('row', 'col'))]
    reduce_sum x0 -> x1, other arithmetic: none -> 12.4 us  [on_device(): gram = pieces.sum(axis=0)]
where the time goes in v2:
time: 517 us
  waiting for transfers between devices  335 us (65%)
  other arithmetic  132 us (26%)
  matrix products  21.5 us (4%)
  between operations  16.1 us (3%)
  local copies, waits for them, and re-layouts  11.1 us (2%)
    all_gather x1, waiting for transfers between devices, on_device(): pieces = lax.all_gather(local_gram, ('row', 'col'), axis=0, tiled=False)  194 us
    psum x1, waiting for transfers between devices, on_device(): summed = lax.psum(local_terms, ('row', 'col'))  142 us
    another operation x14, other arithmetic, on_device(): factor = jnp.linalg.cholesky(gram / npw_total)  78.7 us
    another operation x4, other arithmetic, on_device(): lax.linalg.triangular_solve(factor, predicted, left_side=True, lower=True)  41 us
    reduce_sum x1, other arithmetic, on_device(): gram = pieces.sum(axis=0)  12.4 us
    another operation x12, local copies, waits for them, and re-layouts  10.6 us
  transfers between devices with their start and end apart: 2, of which 2 were waited for; matrix products, arithmetic and copies ran while one was open for 0% of the time, Pallas kernels for 0%

profile of v2, /device:TPU:0, one launch (start us, length us, event | category | flops | bytes accessed | tf_op | source)
XLA Modules:
  0.0 516.7 jit_solution(13874570034546084437)
XLA Ops:
  6.5 3.0 fusion.11
  9.6 3.0 fusion.14
  12.6 3.0 fusion.19
  15.6 141.7 %all-reduce.4.cloned.1.call-done = (f32[512,512]{1,0:T(8,128)}, f32[512,512]{1,0:T(8,128)}, f32[512,512]{1,0:T(8,128)}) async-done(((f32[512,512]{1,0:T(8,128)}, f32[512,512]{1,0:T(8,128)}, f32[512,512]{1,0:T(8,128)}), (f32[512,512]{1,0:T(8,128)}, f32[512,512]{1,0:T(8,128)}, f32[512,512]{1,0:T(8,128)})) %all-reduce.4.cloned.1.call-update) | async-done | bytes 3145744 | tf_op jit(solution)/shard_map/psum | solution.py:14
  157.3 2.3 convolution_multiply_fusion.2
  159.6 2.3 fusion.1
  161.8 2.3 fusion
  164.1 2.0 fusion.61
  166.1 193.6 %all-gather.3.cloned.1.call-done = f32[16384,512]{1,0:T(8,128)} async-done(((f32[512,512]{1,0:T(8,128)}), f32[16384,512]{1,0:T(8,128)}) %all-gather.3.cloned.1.call-update) | async-done | bytes 33554448 | tf_op jit(solution)/shard_map/all_gather | solution.py:21
  359.7 12.4 %reduce_sum.11 = f32[512,512]{1,0:T(8,128)S(1)} reduce(f32[32,512,512]{2,1,0:T(8,128)} %bitcast.70, f32[]{:T(128)} %constant.149.clone.1), dimensions={0}, to_apply=%region_3.0 | reduce | flops 8126464 | bytes 34603012 | tf_op jit(solution)/shard_map/reduce_sum | solution.py:22
  372.2 0.3 copy.3
  372.5 0.2 fusion.2
  372.8 11.7 %cholesky.104 = f32[128,128]{1,0:T(8,128)S(1)} custom-call(f32[128,128]{1,0:T(8,128)S(1)} %cholesky.266), custom_call_target="Cholesky" | custom-call | tf_op jit(solution)/shard_map/jit(cholesky)/cholesky | solution.py:23
  384.5 0.1 cholesky.224
  384.7 9.8 %custom-call.30 = f32[1,128,128]{1,2,0:T(8,128)S(1)} custom-call(f32[1,128,128]{2,1,0:T(8,128)S(1)} %get-tuple-element.35), custom_call_target="InvertDiagBlocksLowerTriangular" | custom-call | tf_op jit(solution)/shard_map/jit(cholesky)/cholesky | solution.py:23
  394.5 0.3 constant_dynamic-update-slice_fusion.3
  394.8 0.3 convolution_subtract_fusion
  395.2 11.7 %cholesky.217 = f32[128,128]{1,0:T(8,128)S(1)} custom-call(f32[128,128]{1,0:T(8,128)S(1)} %cholesky.270), custom_call_target="Cholesky" | custom-call | tf_op jit(solution)/shard_map/jit(cholesky)/cholesky | solution.py:23
  406.9 10.0 %custom-call.31 = f32[1,128,128]{1,2,0:T(8,128)S(1)} custom-call(f32[1,128,128]{2,1,0:T(8,128)S(1)} %get-tuple-element.32), custom_call_target="InvertDiagBlocksLowerTriangular" | custom-call | tf_op jit(solution)/shard_map/jit(cholesky)/cholesky | solution.py:23
  416.9 0.3 convolution_dynamic-update-slice_fusion
  417.2 0.4 convolution_subtract_fusion.1
  417.6 11.7 %cholesky.238 = f32[128,128]{1,0:T(8,128)S(1)} custom-call(f32[128,128]{1,0:T(8,128)S(1)} %cholesky.275), custom_call_target="Cholesky" | custom-call | tf_op jit(solution)/shard_map/jit(cholesky)/cholesky | solution.py:23
  429.3 0.7 compare_reduce_fusion.1
  430.0 9.8 %custom-call.32 = f32[1,128,128]{1,2,0:T(8,128)S(1)} custom-call(f32[1,128,128]{2,1,0:T(8,128)S(1)} %get-tuple-element.29), custom_call_target="InvertDiagBlocksLowerTriangular" | custom-call | tf_op jit(solution)/shard_map/jit(cholesky)/cholesky | solution.py:23
  439.9 0.2 convolution_dynamic-update-slice_fusion.1
  440.1 0.4 convolution_subtract_fusion.5
  440.5 11.7 %cholesky.255 = f32[128,128]{1,0:T(8,128)S(1)} custom-call(f32[128,128]{1,0:T(8,128)S(1)} %convolution_subtract_fusion.5), custom_call_target="Cholesky" | custom-call | tf_op jit(solution)/shard_map/jit(cholesky)/cholesky | solution.py:23
  452.2 0.6 compare_reduce_fusion
  452.8 0.7 compare_reduce_fusion.2
  456.1 0.1 select_select_fusion
  456.2 10.9 %while.1 = (s32[]{:T(128)}, f32[512,512]{1,0:T(8,128)S(1)}, s32[4,2]{0,1:T(2,128)S(1)}, f32[4,128,128]{2,1,0:T(8,128)}, s32[]{:T(128)}) while((s32[]{:T(128)}, f32[512,512]{1,0:T(8,128)S(1)}, s32[4,2]{0,1:T(2,128)S(1)}, f32[4,128,128]{2,1,0:T(8,128)}, s32[]{:T(128)}) %tuple.27), condition=%wide.while_cond, body=%wide.while_body.sunk | while | flops 2 | bytes 132705 | solution.py:24
  456.6 0.6 fusion.70
  457.2 2.0 bitcast_dynamic-update-slice_fusion.2
  459.2 0.6 fusion.70
  459.8 2.0 bitcast_dynamic-update-slice_fusion.2
  461.9 0.6 fusion.70
  462.5 2.0 bitcast_dynamic-update-slice_fusion.2
  464.5 0.6 fusion.70
  465.1 2.0 bitcast_dynamic-update-slice_fusion.2
  467.1 40.1 %custom-call.33 = f32[4,128,128]{1,2,0:T(8,128)S(1)} custom-call(f32[4,128,128]{2,1,0:T(8,128)} %get-tuple-element.12), custom_call_target="InvertDiagBlocksLowerTriangular" | custom-call | tf_op jit(solution)/shard_map/triangular_solve | solution.py:24
  507.2 0.3 fusion.48
  507.5 0.2 convolution_subtract_fusion.3
  507.7 0.3 fusion.47
  508.0 0.3 convolution_subtract_fusion.2
  508.3 0.3 fusion.45
  508.6 0.3 convolution_subtract_fusion.4
  508.9 0.3 fusion.44
  509.2 0.7 pad_maximum_fusion
  (18 shorter events, 0.5 us)
Async XLA Ops:
  6.5 150.8 %all-reduce.4.cloned.1.call-start = ((), (), s32[]{:S(2)}) async-start(), calls=%async_computation.1 | async-start | bytes 6291456 | tf_op jit(solution)/shard_map/psum | solution.py:14
  15.6 344.2 %all-gather.3.cloned.1.call-start = ((), (), s32[]{:S(2)}) async-start(), calls=%async_computation | async-start | bytes 34603008 | tf_op jit(solution)/shard_map/all_gather | solution.py:21
Sparse Core Ops, SparseCore 0:
  15.7 141.5 all-reduce.3
  166.2 193.4 all-gather.2
